TPU v7x, 32 devices: a whole 2x2x4 slice. The times are simulated.
32 devices in a mesh: lag: 16 (over z, y, x), row: 2 (over core).
Axes of the slice: x: 2, y: 2, z: 4, core: 2. Of those that a mesh axis runs over, the one named last changes fastest.
Arguments:
- blocks: bfloat16 [32, 2048, 2048], P('lag', 'row'), may hold values from -0.03125 to 0.03125
- history: bfloat16 [32, 2048, 128], P('lag'), may hold values from -6 to 6
- excitation: float32 [2, 2048, 128], P(None, 'row'), may hold values from -6 to 6
- self_inverse: float32 [2048, 2048], P('lag', 'row'), may hold values from -2 to 2
Outputs:
- currents: float32 [2, 2048, 128], P(None, 'lag')
All inputs are finite; a program needn't handle non-finite values.
Results may differ from a plain program's by a relative error of at most 0.0003.
Values may be sent and summed in bfloat16 or wider, within the bound.
A program may use at most 64 MiB of HBM per device.

v0:
```python
import jax
import jax.numpy as jnp
from jax import lax
from jax.sharding import PartitionSpec as P

STEPS = 2


def shifted(block, axis, distance):
    devices = range(lax.axis_size(axis))
    route = [(i - distance, i) for i in devices if i - distance in devices]
    return lax.ppermute(block, axis, route)


def shards(blocks, history, excitation, self_inverse):
    lag_index = lax.axis_index("lag")
    past = history
    inverse_full = lax.all_gather(self_inverse, "row", axis=1, tiled=True)
    results = []
    for marker in range(STEPS):
        partial_value = jnp.einsum("lpq,lqc->pc", blocks, past, preferred_element_type=jnp.float32)
        summed = lax.psum(partial_value, "lag")
        residual = excitation[marker] - summed
        full_residual = lax.all_gather(residual, "row", axis=0, tiled=True)
        solved = jnp.dot(
            inverse_full,
            full_residual,
            precision=lax.Precision.HIGHEST,
            preferred_element_type=jnp.float32,
        )
        results.append(solved)
        if marker + 1 < STEPS:
            newest = lax.all_gather(solved.astype(jnp.bfloat16), "lag", axis=0, tiled=True)
            moved = shifted(past[-1:], "lag", 1)
            leading = jnp.where(lag_index == 0, newest[None], moved)
            past = jnp.concatenate([leading, past[:-1]], axis=0)
    return jnp.stack(results)


def solution(mesh):
    return jax.shard_map(
        shards,
        mesh=mesh,
        in_specs=(
            P("lag", "row", None),
            P("lag", None, None),
            P(None, "row", None),
            P("lag", "row"),
        ),
        out_specs=P(None, "lag", None),
        check_vma=False,
    )
```

profile of v0, /device:TPU:7, one launch (start us, length us, event | category | flops | bytes accessed | tf_op | source)
XLA Modules:
  0.0 316.0 jit_solution(17562383805654095)
XLA Ops:
  7.4 6.9 %convolution_bitcast_fusion.1 = f32[1024,128]{1,0:T(8,128)} fusion(bf16[2,1024,2048]{2,1,0:T(8,128)(2,1)} %param.4, bf16[2,2048,128]{2,1,0:T(8,128)(2,1)} %param.5), kind=kOutput, calls=%fused_computation.1 | convolution fusion | flops 1073741824 | bytes 9961472 | tf_op jit(solution)/shard_map/lpq,lqc->pc/dot_general | solution.py:21
  14.3 0.0 all-gather.6.cloned.1.call-start
  14.3 0.5 all-gather.6.cloned.1.call-update
  14.9 0.0 all-gather.4.cloned.1.call-start
  14.9 107.5 %all-reduce.3.cloned.1.call-done = f32[1024,128]{1,0:T(8,128)} async-done(((f32[1024,128]{1,0:T(8,128)}), f32[1024,128]{1,0:T(8,128)}) %all-reduce.3.cloned.1.call-update) | async-done | bytes 524304 | tf_op jit(solution)/shard_map/psum | solution.py:22
  122.4 1.9 bitcast_subtract_fusion.1
  124.3 0.0 all-gather.4.cloned.1.call-update
  124.4 0.0 all-reduce.5.cloned.1.call-start
  124.4 0.1 fusion.4
  124.5 0.2 copy.8
  124.7 2.4 collective-permute-start
  127.1 0.2 copy.9
  127.3 0.0 all-gather.6.cloned.1.call-done
  127.4 8.1 %all-gather.4.cloned.1.call-done = f32[2048,128]{1,0:T(8,128)} async-done(((f32[1024,128]{1,0:T(8,128)}), f32[2048,128]{1,0:T(8,128)}) %all-gather.4.cloned.1.call-update) | async-done | bytes 1048592 | tf_op jit(solution)/shard_map/all_gather | solution.py:24
  135.4 3.4 %bitcast_convert_fusion = (bf16[128,128]{0,1:T(8,128)(2,1)S(1)}, f32[128,128]{1,0:T(8,128)S(1)}) fusion(f32[2048,128]{1,0:T(8,128)} %all-gather.4.cloned.1.call-done, f32[128,2048]{1,0:T(8,128)} %all-gather.6.cloned.1.call-done), kind=kOutput, calls=%fused_computation.10 | convolution fusion | flops 402669568 | bytes 2195456 | tf_op jit(solution)/shard_map/dot_general | solution.py:25
  138.8 28.9 %all_gather.14 = bf16[2048,128]{0,1:T(8,128)(2,1)S(1)} all-gather(bf16[128,128]{0,1:T(8,128)(2,1)S(1)} %get-tuple-element.7), channel_id=1, replica_groups=mesh['lag'=16,'row'=2] {'lag'}, dimensions={0}, use_global_device_ids=true | all-gather | bytes 557056 | tf_op jit(solution)/shard_map/all_gather | solution.py:33
  167.6 0.1 bitcast_select_fusion
  167.7 6.6 %convolution_bitcast_fusion = f32[1024,128]{1,0:T(8,128)} fusion(bf16[2,1024,2048]{2,1,0:T(8,128)(2,1)} %param.4, bf16[1,2048,128]{1,2,0:T(8,128)(2,1)S(1)} %copy.9, bf16[1,2048,128]{1,2,0:T(8,128)(2,1)S(1)} %bitcast_select_fusion), kind=kOutput, calls=%fused_computation | convolution fusion | flops 1074266112 | bytes 9961472 | tf_op jit(solution)/shard_map/lpq,lqc->pc/dot_general | solution.py:21
  174.3 0.0 all-gather.8.cloned.1.call-start
  174.4 117.2 %all-reduce.5.cloned.1.call-done = f32[1024,128]{1,0:T(8,128)} async-done(((f32[1024,128]{1,0:T(8,128)}), f32[1024,128]{1,0:T(8,128)}) %all-reduce.5.cloned.1.call-update) | async-done | bytes 524304 | tf_op jit(solution)/shard_map/psum | solution.py:22
  291.6 1.9 bitcast_subtract_fusion
  293.6 11.1 %all-gather.8.cloned.1.call-done = f32[2048,128]{1,0:T(8,128)} async-done(((f32[1024,128]{1,0:T(8,128)}), f32[2048,128]{1,0:T(8,128)}) %all-gather.8.cloned.1.call-update) | async-done | bytes 1048592 | tf_op jit(solution)/shard_map/all_gather | solution.py:24
  304.6 3.0 convolution_bitcast_fusion.2
  307.7 0.8 copy.7
  (12 shorter events, 0.1 us)
Async XLA Ops:
  7.4 117.1 %copy-start.2 = (bf16[2,2048,128]{2,1,0:T(8,128)(2,1)S(1)}, bf16[2,2048,128]{2,1,0:T(8,128)(2,1)}, u32[]{:S(2)}) copy-start(bf16[2,2048,128]{2,1,0:T(8,128)(2,1)} %param.5) | copy-start | bytes 3145732
  7.4 115.1 %copy-start.1 = (f32[2,1024,128]{2,1,0:T(8,128)S(1)}, f32[2,1024,128]{2,1,0:T(8,128)}, u32[]{:S(2)}) copy-start(f32[2,1024,128]{2,1,0:T(8,128)} %param.6) | copy-start | bytes 3145732
  7.4 115.1 %all-reduce.3.cloned.1.call-start = ((), (), s32[]{:S(2)}) async-start(), calls=%async_computation | async-start | bytes 1048576 | tf_op jit(solution)/shard_map/psum | solution.py:22
  14.3 113.1 %all-gather.6.cloned.1.call-start = ((), (), s32[]{:S(2)}) async-start(), calls=%async_computation.2 | async-start | bytes 1572864 | tf_op jit(solution)/shard_map/all_gather | solution.py:18
  14.9 120.6 %all-gather.4.cloned.1.call-start = ((), (), s32[]{:S(2)}) async-start(), calls=%async_computation.1 | async-start | bytes 1572864 | tf_op jit(solution)/shard_map/all_gather | solution.py:24
  124.4 167.3 %all-reduce.5.cloned.1.call-start = ((), (), s32[]{:S(2)}) async-start(), calls=%async_computation.3 | async-start | bytes 1048576 | tf_op jit(solution)/shard_map/psum | solution.py:22
  124.7 42.9 %collective-permute-start = (bf16[1,2048,128]{1,2,0:T(8,128)(2,1)S(1)}, bf16[1,2048,128]{1,2,0:T(8,128)(2,1)S(1)}, u32[]{:S(2)}, u32[]{:S(2)}) collective-permute-start(bf16[1,2048,128]{1,2,0:T(8,128)(2,1)S(1)} %copy.8), channel_id=1, source_target_pairs={{0,2},{2,4},{4,6},{6,8},{8,10},{10,12},{12,14},{14,16},{16,18},{18... | collective-permute-start | bytes 1572872 | tf_op jit(solution)/shard_map/ppermute | solution.py:12
  167.7 136.9 %copy-start = (f32[128,2048]{1,0:T(8,128)S(1)}, f32[128,2048]{1,0:T(8,128)}, u32[]{:S(2)}) copy-start(f32[128,2048]{1,0:T(8,128)} %all-gather.6.cloned.1.call-done) | copy-start | bytes 3145732
  174.3 130.3 %all-gather.8.cloned.1.call-start = ((), (), s32[]{:S(2)}) async-start(), calls=%async_computation.4 | async-start | bytes 1572864 | tf_op jit(solution)/shard_map/all_gather | solution.py:24
Sparse Core Ops, SparseCore 0:
  14.4 107.9 all-reduce.2
  174.5 117.1 all-reduce.4
Sparse Core Ops, SparseCore 1:
  16.3 10.8 all-gather.5
  124.5 10.9 all-gather.3
  293.6 10.9 all-gather.7
where the time goes:
time: 317 us; the launch traced here: 316 us
  waiting for transfers between devices  244 us (77%)
  blocking collectives  28.9 us (9%)
  matrix products  19.9 us (6%)
  between operations  15.1 us (5%)
  other arithmetic  3.87 us (1%)
    psum x2, waiting for transfers between devices, shards(): summed = lax.psum(partial_value, 'lag')  225 us
    all_gather x1, blocking collectives, shards(): lax.all_gather(solved.astype(jnp.bfloat16), 'lag', axis=0, tiled=True)  28.9 us
    all_gather x2, waiting for transfers between devices, shards(): full_residual = lax.all_gather(residual, 'row', axis=0, tiled=True)  19.1 us
    dot_general x2, matrix products, shards(): jnp.einsum('lpq,lqc->pc', blocks, past, preferred_element_type=jnp.float32)  13.5 us
    dot_general x2, matrix products, shards(): jnp.dot(inverse_full, full_residual, precision=lax.Precision.HIGHEST, pre...  6.39 us
  transfers between devices with their start and end apart: 6, of which 4 were waited for; matrix products, arithmetic and copies ran while one was open for 2% of the time, Pallas kernels for 0%

commit v1 on v0

v1 whole, which is shorter than its diff:
```python
import functools

import jax
import jax.numpy as jnp
from jax import lax
from jax.experimental import pallas as pl
from jax.experimental.pallas import tpu as pltpu
from jax.sharding import PartitionSpec as P

F32 = jnp.float32
BF16 = jnp.bfloat16


def split_of(lags):
    outer = 1
    while outer * outer * 4 <= lags and lags % (outer * 2) == 0:
        outer *= 2
    return outer, lags // outer


def kernel(A, B, R, G, blocks, history, excitation, inverse, out, *scratch):
    (bvm, hist, hprev, exc, inv, pbuf, rs1, mid, rs2, ag, ex, cbuf, gbuf, dbuf, dpiece, ld, ldb, hs, hr, hds, hdr,
     s1, r1, s2, r2, zs, zr, xs, xr, es, er, gs, gr, gds, gdr, ds, dr) = scratch
    L = A * B
    nloc = hist.shape[0]
    s, C = ag.shape[2], ag.shape[3]
    rows = A * s
    i = lax.axis_index("lag")
    r = lax.axis_index("row")
    a, b = i // B, lax.rem(i, B)
    mine = b * A + a

    def at(lag, row):
        return {"lag": lag, "row": row}

    def plane(k):
        return at(a * B + lax.rem(b + k, B), r)

    def line(k):
        return at(lax.rem(a + k, A) * B + b, r)

    def beside(k):
        return at(i, lax.rem(r + k, R))

    def put(src, dst, ss, rs, to):
        c = pltpu.make_async_remote_copy(src_ref=src, dst_ref=dst, send_sem=ss, recv_sem=rs, device_id=to, device_id_type=pl.DeviceIdType.MESH)
        c.start()
        return c

    def got(dst, ss, rs, to):
        pltpu.make_async_remote_copy(src_ref=dst, dst_ref=dst, send_sem=ss, recv_sem=rs, device_id=to, device_id_type=pl.DeviceIdType.MESH).wait_recv()

    hcopy = pltpu.make_async_copy(history, hist, ld.at[0])
    hcopy.start()
    loads = []
    for k in range(1, B + 1):
        g = pl.multiple_of(lax.rem(b + k, B) * rows, rows)
        c = pltpu.make_async_copy(blocks.at[:, pl.ds(g, rows)], bvm.at[:, pl.ds(g, rows)], ldb.at[k - 1])
        c.start()
        loads.append(c)
    ecopy = pltpu.make_async_copy(excitation.at[:, mine], exc, ld.at[1])
    ecopy.start()
    icopy = pltpu.make_async_copy(inverse, inv, ld.at[2])
    icopy.start()

    barrier = pltpu.get_barrier_semaphore()

    def hello(to):
        pl.semaphore_signal(barrier, inc=1, device_id=to, device_id_type=pl.DeviceIdType.MESH)

    for k in range(1, B):
        hello(plane(k))
    for k in range(1, A):
        hello(line(k))
    for k in range(1, R):
        hello(beside(k))

    @pl.when(i > 0)
    def _():
        hello(at(i - 1, r))
        hello(at(0, r))

    @pl.when(i < L - 1)
    def _():
        hello(at(i + 1, r))

    @pl.when(i == 0)
    def _():
        for j in range(1, L):
            hello(at(j, r))

    root, last = 1 - (i + L - 1) // L, (i + 1) // L
    pl.semaphore_wait(barrier, A + B + R - 3 + 2 * (1 - root) + (1 - last) + (L - 1) * root)

    sends = []

    def scatter_first(t, operand_of, before):
        for k in range(1, B + 1):
            before(k)
            to = lax.rem(b + k, B)
            g = pl.multiple_of(to * rows, rows)
            total = jnp.dot(bvm[0, pl.ds(g, rows), :], operand_of(0), preferred_element_type=F32)
            for l in range(1, nloc):
                total += jnp.dot(bvm[l, pl.ds(g, rows), :], operand_of(l), preferred_element_type=F32)
            for n in range(A):
                pbuf[t, to, n] = total[n * s:(n + 1) * s]
            if k < B:
                sends.append(put(pbuf.at[t, to], rs1.at[t, k - 1], s1.at[t, k - 1], r1.at[t, k - 1], plane(k)))

    def scatter_second(t):
        for k in range(1, B):
            got(rs1.at[t, k - 1], s1.at[t, k - 1], r1.at[t, k - 1], plane(k))
        for k in range(1, A + 1):
            to = lax.rem(a + k, A)
            total = pbuf[t, b, to]
            for n in range(B - 1):
                total += rs1[t, n, to]
            mid[t, k - 1] = total
            if k < A:
                sends.append(put(mid.at[t, k - 1], rs2.at[t, k - 1], s2.at[t, k - 1], r2.at[t, k - 1], line(k)))
        total = mid[t, A - 1]
        for k in range(1, A):
            got(rs2.at[t, k - 1], s2.at[t, k - 1], r2.at[t, k - 1], line(k))
            total += rs2[t, k - 1]
        return total

    def gather(t):
        for k in range(1, A):
            sends.append(put(ag.at[t, mine], ag.at[t, mine], zs.at[t, k - 1], zr.at[t, k - 1], line(k)))

        def spread(n):
            piece = b * A + lax.rem(a + A - n, A)
            if n:
                got(ag.at[t, piece], zs.at[t, n - 1], zr.at[t, n - 1], line(n))
            for k in range(1, B):
                sends.append(put(ag.at[t, piece], ag.at[t, piece], xs.at[t, n, k - 1], xr.at[t, n, k - 1], plane(k)))

        for n in range(A):
            spread(n)
        for n in range(A):
            for k in range(1, B):
                piece = lax.rem(b + B - k, B) * A + lax.rem(a + A - n, A)
                got(ag.at[t, piece], xs.at[t, n, k - 1], xr.at[t, n, k - 1], plane(k))

    def solve(t):
        full = ag[t].reshape(L * s, C)
        ex[t, r] = jnp.dot(inv[...], full, precision=lax.Precision.HIGHEST, preferred_element_type=F32)
        for k in range(1, R):
            sends.append(put(ex.at[t, r], ex.at[t, r], es.at[t, k - 1], er.at[t, k - 1], beside(k)))
        for k in range(1, R):
            got(ex.at[t, lax.rem(r + R - k, R)], es.at[t, k - 1], er.at[t, k - 1], beside(k))
        total = ex[t, 0]
        for n in range(1, R):
            total += ex[t, n]
        out[t] = total
        return total

    def before(k):
        if k == 1:
            hcopy.wait()
        loads[k - 1].wait()

    scatter_first(0, lambda l: hist[l], before)
    part = hprev.shape[0] // R
    share = pl.ds(pl.multiple_of(r * part, part), part)

    @pl.when(i < L - 1)
    def _():
        put(hist.at[nloc - 1, share], hprev.at[share], hs.at[0], hr.at[0], at(i + 1, r))

    ecopy.wait()
    icopy.wait()
    ag[0, mine] = exc[0] - scatter_second(0)
    gather(0)
    current = solve(0).astype(BF16)
    h = cbuf.shape[1]
    for n in range(G):
        cbuf[n] = current[n * h:(n + 1) * h]
    which = r if G > 1 else 0

    @pl.when(i > 0)
    def _():
        put(cbuf.at[which], gbuf.at[i, which], gs.at[0], gr.at[i], at(0, r))

    @pl.when(i > 0)
    def _():
        got(hprev.at[share], hs.at[0], hr.at[0], at(i - 1, r))

    @pl.when(i == 0)
    def _():
        hprev[...] = jnp.zeros_like(hprev)

    @pl.when(i > 0)
    def _():
        for k in range(1, R):
            put(hprev.at[share], hprev.at[share], hds.at[k - 1], hdr.at[k - 1], beside(k))
        for k in range(1, R):
            theirs = pl.ds(pl.multiple_of(lax.rem(r + R - k, R) * part, part), part)
            got(hprev.at[theirs], hds.at[k - 1], hdr.at[k - 1], beside(k))

    scatter_first(1, lambda l: hist[l - 1] if l else hprev[...], lambda k: None)

    @pl.when(i == 0)
    def _():
        gbuf[0, which] = cbuf[which]
        for j in range(1, L):
            got(gbuf.at[j, which], gs.at[0], gr.at[j], at(j, r))
        if G > 1:
            swaps = [put(gbuf.at[:, r], gbuf.at[:, r], gds.at[k - 1], gdr.at[k - 1], beside(k)) for k in range(1, R)]
            for k in range(1, R):
                got(gbuf.at[:, lax.rem(r + R - k, R)], gds.at[k - 1], gdr.at[k - 1], beside(k))
        newest = gbuf[...].reshape(L * G * h, C)
        for n in range(B):
            late = jnp.dot(bvm[0, n * rows:(n + 1) * rows, :], newest, preferred_element_type=F32)
            for m in range(A):
                dbuf[n * A + m] = late[m * s:(m + 1) * s]
                j = m * B + n
                if j:
                    put(dbuf.at[n * A + m], dpiece, ds.at[j], dr.at[0], at(j, r))
        dpiece[...] = dbuf[0]
        for j in range(1, L):
            pltpu.make_async_remote_copy(src_ref=dpiece, dst_ref=dpiece, send_sem=ds.at[j], recv_sem=dr.at[0], device_id=at(j, r), device_id_type=pl.DeviceIdType.MESH).wait_send()
        if G > 1:
            for c in swaps:
                c.wait_send()

    given = exc[1] - scatter_second(1)

    @pl.when(i > 0)
    def _():
        got(dpiece, ds.at[0], dr.at[0], at(0, r))

    ag[1, mine] = given - dpiece[...]
    gather(1)
    solve(1)

    for c in sends:
        c.wait_send()

    def left(src, ss, rs, to):
        pltpu.make_async_remote_copy(src_ref=src, dst_ref=src, send_sem=ss, recv_sem=rs, device_id=to, device_id_type=pl.DeviceIdType.MESH).wait_send()

    @pl.when(i < L - 1)
    def _():
        left(hprev.at[share], hs.at[0], hr.at[0], at(i + 1, r))

    @pl.when(i > 0)
    def _():
        left(cbuf.at[which], gs.at[0], gr.at[0], at(0, r))
        for k in range(1, R):
            left(hprev.at[share], hds.at[k - 1], hdr.at[k - 1], beside(k))


def solution(mesh):
    L, R = mesh.shape["lag"], mesh.shape["row"]
    A, B = split_of(L)

    def shards(blocks, history, excitation, inverse):
        nloc, pr, p = blocks.shape
        steps, _, C = excitation.shape
        q = inverse.shape[0]
        s = pr // L
        G = R if (q // R) % 16 == 0 else 1
        dma = pltpu.SemaphoreType.DMA
        return pl.pallas_call(
            functools.partial(kernel, A, B, R, G),
            out_shape=jax.ShapeDtypeStruct((steps, q, C), F32),
            in_specs=[pl.BlockSpec(memory_space=pl.ANY)] * 4,
            out_specs=pl.BlockSpec(memory_space=pltpu.VMEM),
            scratch_shapes=[
                pltpu.VMEM((nloc, pr, p), BF16),
                pltpu.VMEM((nloc, p, C), BF16),
                pltpu.VMEM((p, C), BF16),
                pltpu.VMEM((steps, s, C), F32),
                pltpu.VMEM((q, pr), F32),
                pltpu.VMEM((steps, B, A, s, C), F32),
                pltpu.VMEM((steps, B - 1, A, s, C), F32),
                pltpu.VMEM((steps, A, s, C), F32),
                pltpu.VMEM((steps, A - 1, s, C), F32),
                pltpu.VMEM((steps, L, s, C), F32),
                pltpu.VMEM((steps, R, q, C), F32),
                pltpu.VMEM((G, q // G, C), BF16),
                pltpu.VMEM((L, G, q // G, C), BF16),
                pltpu.VMEM((L, s, C), F32),
                pltpu.VMEM((s, C), F32),
                dma((3,)), dma((B,)), dma((1,)), dma((1,)), dma((R - 1,)), dma((R - 1,)),
                dma((steps, B - 1)), dma((steps, B - 1)), dma((steps, A - 1)), dma((steps, A - 1)),
                dma((steps, A - 1)), dma((steps, A - 1)), dma((steps, A, B - 1)), dma((steps, A, B - 1)),
                dma((steps, R - 1)), dma((steps, R - 1)),
                dma((1,)), dma((L,)), dma((R - 1,)), dma((R - 1,)), dma((L,)), dma((1,)),
            ],
            compiler_params=pltpu.CompilerParams(collective_id=0, has_side_effects=True, vmem_limit_bytes=60 * 1024 * 1024),
        )(blocks, history, excitation.reshape(steps, L, s, C), inverse)

    return jax.shard_map(
        shards,
        mesh=mesh,
        in_specs=(P("lag", "row", None), P("lag", None, None), P(None, "row", None), P("lag", "row")),
        out_specs=P(None, "lag", None),
        check_vma=False,
    )
```

time: 317 us -> 65.8 us (0.21)
  waiting for transfers between devices: 244 us -> 0 us
  Pallas kernels: 0 us -> 64 us
  blocking collectives: 28.9 us -> 0 us
  matrix products: 19.9 us -> 0 us
  between operations: 15.1 us -> 0.01 us
  other arithmetic: 3.87 us -> 0 us
    psum x2 -> x0, waiting for transfers between devices: 225 us -> none  [shards(): summed = lax.psum(partial_value, 'lag')]
    pallas_call x0 -> x1, Pallas kernels: none -> 64 us  [shards(): pl.pallas_call(functools.partial(kernel, A, B, R, G), out_shape=jax.Shape...]
    all_gather x1 -> x0, blocking collectives: 28.9 us -> none  [shards(): lax.all_gather(solved.astype(jnp.bfloat16), 'lag', axis=0, tiled=True)]
    dot_general x4 -> x0, matrix products: 19.9 us -> none  [the longest x2 13.5 us: shards(): jnp.einsum('lpq,lqc->pc', blocks, past, preferred_element_type=jnp.float32)]
    all_gather x3 -> x0, waiting for transfers between devices: 19.2 us -> none  [the longest x2 19.1 us: shards(): full_residual = lax.all_gather(residual, 'row', axis=0, tiled=True)]
    sub x2 -> x0, other arithmetic: 3.8 us -> none  [shards(): residual = excitation[marker] - summed]
  transfers between devices with their start and end apart: 6 -> 0, of which waited for: 4 -> 0; matrix products, arithmetic and copies ran while one was open for 2% -> 0% of each run, Pallas kernels for 0% -> 0%
where the time goes in v1:
time: 65.8 us; the launch traced here: 65.6 us
  Pallas kernels  64 us (97%)
  local copies, waits for them, and re-layouts  1.57 us (2%)
    pallas_call x1, Pallas kernels, shards(): pl.pallas_call(functools.partial(kernel, A, B, R, G), out_shape=jax.Shape...  64 us
    unnamed x1, local copies, waits for them, and re-layouts  1.57 us

profile of v1, /device:TPU:7, one launch (start us, length us, event | category | flops | bytes accessed | tf_op | source)
XLA Modules:
  0.0 65.6 jit_solution(15904656424359937956)
XLA Ops:
  0.0 64.0 %shard_map.46 = f32[2,128,128]{2,1,0:T(8,128)} custom-call(bf16[2,1024,2048]{2,1,0:T(8,128)(2,1)} %blocks.1, bf16[2,2048,128]{2,1,0:T(8,128)(2,1)} %history.1, f32[2,16,64,128]{3,2,1,0:T(8,128)} %bitcast.1, f32[128,1024]{1,0:T(8,128)} %inverse.1), custom_call_target="tpu_custom_call" | custom-call | tf_op jit(solution)/shard_map/pallas_call | solution.py:265
  64.0 1.6 %copy.6 = f32[2,128,128]{2,1,0:T(8,128)} copy(f32[2,128,128]{2,1,0:T(8,128)} %shard_map.46) | data formatting | bytes 262144

commit v2 on v1

v2 whole, which is shorter than its diff:
```python
import functools

import jax
import jax.numpy as jnp
from jax import lax
from jax.experimental import pallas as pl
from jax.experimental.pallas import tpu as pltpu
from jax.sharding import PartitionSpec as P

F32 = jnp.float32
BF16 = jnp.bfloat16


def split_of(lags):
    outer = 1
    while outer * outer * 4 <= lags and lags % (outer * 2) == 0:
        outer *= 2
    return outer, lags // outer


def kernel(A, B, R, G, blocks, history, excitation, inverse, out, *scratch):
    (bvm, hist, exc, inv, pbuf, rs1, mid, rs2, ag, ex, cbuf, gbuf, dbuf, dpiece, ld, ldb, hs, hr, hds, hdr,
     s1, r1, s2, r2, zs, zr, xs, xr, es, er, gs, gr, gds, gdr, ds, dr) = scratch
    L = A * B
    nloc = bvm.shape[0]
    hprev = hist.at[0]
    s, C = ag.shape[2], ag.shape[3]
    rows = A * s
    i = lax.axis_index("lag")
    r = lax.axis_index("row")
    a, b = i // B, lax.rem(i, B)
    mine = b * A + a

    def at(lag, row):
        return {"lag": lag, "row": row}

    def flipped(k):
        place, step = b, 1
        while step < B:
            place = place + (k // step % 2) * (step - 2 * step * lax.rem(b // step, 2))
            step *= 2
        return place

    def plane(k):
        return at(a * B + flipped(k), r)

    def line(k):
        return at(lax.rem(a + k, A) * B + b, r)

    def beside(k):
        return at(i, lax.rem(r + k, R))

    def put(src, dst, ss, rs, to):
        c = pltpu.make_async_remote_copy(src_ref=src, dst_ref=dst, send_sem=ss, recv_sem=rs, device_id=to, device_id_type=pl.DeviceIdType.MESH)
        c.start()
        return c

    def got(dst, ss, rs, to):
        pltpu.make_async_remote_copy(src_ref=dst, dst_ref=dst, send_sem=ss, recv_sem=rs, device_id=to, device_id_type=pl.DeviceIdType.MESH).wait_recv()

    hcopy = pltpu.make_async_copy(history, hist.at[pl.ds(1, nloc)], ld.at[0])
    hcopy.start()
    for k in range(B - 1, -1, -1):
        g = pl.multiple_of(flipped(k) * rows, rows)
        c = pltpu.make_async_copy(blocks.at[:, pl.ds(g, rows)], bvm.at[:, pl.ds(g, rows)], ldb.at[k])
        c.start()
    ecopy = pltpu.make_async_copy(excitation.at[:, mine], exc, ld.at[1])
    ecopy.start()
    icopy = pltpu.make_async_copy(inverse, inv, ld.at[2])
    icopy.start()

    barrier = pltpu.get_barrier_semaphore()

    def hello(to):
        pl.semaphore_signal(barrier, inc=1, device_id=to, device_id_type=pl.DeviceIdType.MESH)

    for k in range(1, B):
        hello(plane(k))
    for k in range(1, A):
        hello(line(k))
    for k in range(1, R):
        hello(beside(k))

    @pl.when(i > 0)
    def _():
        hello(at(i - 1, r))
        hello(at(0, r))

    @pl.when(i < L - 1)
    def _():
        hello(at(i + 1, r))

    @pl.when(i == 0)
    def _():
        for j in range(1, L):
            hello(at(j, r))

    sends = []
    root, last = 1 - (i + L - 1) // L, (i + 1) // L
    pl.semaphore_wait(barrier, A + B + R - 3 + 2 * (1 - root) + (1 - last) + (L - 1) * root)


    def scatter_first(t, before):
        @pl.loop(0, B)
        def _(step):
            k = B - 1 - step
            before(k)
            to = flipped(k)
            g = pl.multiple_of(to * rows, rows)
            total = jnp.dot(bvm[0, pl.ds(g, rows), :], hist[1 - t], preferred_element_type=F32)
            for l in range(1, nloc):
                total += jnp.dot(bvm[l, pl.ds(g, rows), :], hist[l + 1 - t], preferred_element_type=F32)
            for n in range(A):
                pbuf[t, to, n] = total[n * s:(n + 1) * s]

            @pl.when(k > 0)
            def _():
                @pl.loop(1, A + 1)
                def _(m):
                    n = lax.rem(a + m, A)
                    put(pbuf.at[t, to, n], rs1.at[t, k - 1, n], s1.at[t, k - 1, m - 1], r1.at[t, k - 1, n], plane(k))

    def scatter_second(t):
        for k in range(1, A + 1):
            to = lax.rem(a + k, A)
            for n in range(B - 1, 0, -1):
                got(rs1.at[t, n - 1, to], s1.at[t, n - 1, k - 1], r1.at[t, n - 1, to], plane(n))
            total = pbuf[t, b, to]
            for n in range(B - 1):
                total += rs1[t, n, to]
            mid[t, k - 1] = total
            if k < A:
                sends.append(put(mid.at[t, k - 1], rs2.at[t, k - 1], s2.at[t, k - 1], r2.at[t, k - 1], line(k)))
        total = mid[t, A - 1]
        for k in range(1, A):
            got(rs2.at[t, k - 1], s2.at[t, k - 1], r2.at[t, k - 1], line(k))
            total += rs2[t, k - 1]
        return total

    def gather(t, between):
        for k in range(1, A):
            sends.append(put(ag.at[t, mine], ag.at[t, mine], zs.at[t, k - 1], zr.at[t, k - 1], line(k)))

        def piece_of(k, n):
            return flipped(k) * A + lax.rem(a + A - n, A)

        def spread(n, ks):
            piece = piece_of(0, n)
            for k in ks:
                sends.append(put(ag.at[t, piece], ag.at[t, piece], xs.at[t, n, k - 1], xr.at[t, n, k - 1], plane(k)))

        near = [k for k in range(1, B) if k & (k - 1) == 0]
        far = [k for k in range(1, B) if k & (k - 1)]
        spread(0, near + far)
        for n in range(1, A):
            got(ag.at[t, piece_of(0, n)], zs.at[t, n - 1], zr.at[t, n - 1], line(n))
            spread(n, near)
        for n in range(1, A):
            spread(n, far)
        between()
        total = None
        for k in [0] + near + far:
            if k:
                for n in range(A):
                    got(ag.at[t, piece_of(k, n)], xs.at[t, n, k - 1], xr.at[t, n, k - 1], plane(k))
            if rows % 128 == 0:
                g = pl.multiple_of(flipped(k) * rows, rows)
                term = exact(inv[:, pl.ds(g, rows)], ag[t, pl.ds(flipped(k) * A, A)].reshape(rows, C))
                total = term if total is None else total + term
        if total is None:
            total = exact(inv[...], ag[t].reshape(L * s, C))
        return total

    def exact(left, right):
        return jnp.dot(left, right, precision=lax.Precision.HIGHEST, preferred_element_type=F32)

    def solve(t, between):
        ex[t, r] = gather(t, between)
        for k in range(1, R):
            sends.append(put(ex.at[t, r], ex.at[t, r], es.at[t, k - 1], er.at[t, k - 1], beside(k)))
        for k in range(1, R):
            got(ex.at[t, lax.rem(r + R - k, R)], es.at[t, k - 1], er.at[t, k - 1], beside(k))
        total = ex[t, 0]
        for n in range(1, R):
            total += ex[t, n]
        out[t] = total
        return total

    hcopy.wait()

    def before(k):
        g = pl.multiple_of(flipped(k) * rows, rows)
        pltpu.make_async_copy(blocks.at[:, pl.ds(g, rows)], bvm.at[:, pl.ds(g, rows)], ldb.at[k]).wait()

    scatter_first(0, before)
    part = hist.shape[1] // R
    share = pl.ds(pl.multiple_of(r * part, part), part)

    @pl.when(i < L - 1)
    def _():
        put(hist.at[nloc, share], hprev.at[share], hs.at[0], hr.at[0], at(i + 1, r))

    def given_history():
        @pl.when(i > 0)
        def _():
            got(hprev.at[share], hs.at[0], hr.at[0], at(i - 1, r))

        @pl.when(i == 0)
        def _():
            hprev[...] = jnp.zeros(hist.shape[1:], BF16)

        @pl.when(i > 0)
        def _():
            for k in range(1, R):
                put(hprev.at[share], hprev.at[share], hds.at[k - 1], hdr.at[k - 1], beside(k))
            for k in range(1, R):
                theirs = pl.ds(pl.multiple_of(lax.rem(r + R - k, R) * part, part), part)
                got(hprev.at[theirs], hds.at[k - 1], hdr.at[k - 1], beside(k))

        scatter_first(1, lambda k: None)

    ecopy.wait()
    icopy.wait()
    ag[0, mine] = exc[0] - scatter_second(0)
    current = solve(0, given_history).astype(BF16)
    h = cbuf.shape[1]
    for n in range(G):
        cbuf[n] = current[n * h:(n + 1) * h]
    which = r if G > 1 else 0

    @pl.when(i > 0)
    def _():
        put(cbuf.at[which], gbuf.at[i, which], gs.at[0], gr.at[i], at(0, r))

    @pl.when(i == 0)
    def _():
        gbuf[0, which] = cbuf[which]
        swaps = []

        def swap(j):
            if G > 1:
                for k in range(1, R):
                    swaps.append(put(gbuf.at[j, r], gbuf.at[j, r], gds.at[k - 1, j], gdr.at[k - 1, j], beside(k)))

        swap(0)
        for j in range(1, L):
            got(gbuf.at[j, which], gs.at[0], gr.at[j], at(j, r))
            swap(j)
        if G > 1:
            for j in range(L):
                for k in range(1, R):
                    got(gbuf.at[j, lax.rem(r + R - k, R)], gds.at[k - 1, j], gdr.at[k - 1, j], beside(k))
        hist[0] = gbuf[...].reshape(L * G * h, C)

        @pl.loop(0, B)
        def _(n):
            late = jnp.dot(bvm[0, pl.ds(pl.multiple_of(n * rows, rows), rows), :], hist[0], preferred_element_type=F32)
            for m in range(A):
                dbuf[n * A + m] = late[m * s:(m + 1) * s]

            @pl.loop(0, A)
            def _(m):
                j = m * B + n

                @pl.when(j > 0)
                def _():
                    put(dbuf.at[n * A + m], dpiece, ds.at[j], dr.at[0], at(j, r))

        dpiece[...] = dbuf[0]
        for j in range(1, L):
            pltpu.make_async_remote_copy(src_ref=dpiece, dst_ref=dpiece, send_sem=ds.at[j], recv_sem=dr.at[0], device_id=at(j, r), device_id_type=pl.DeviceIdType.MESH).wait_send()
        for c in swaps:
            c.wait_send()

    given = exc[1] - scatter_second(1)

    @pl.when(i > 0)
    def _():
        got(dpiece, ds.at[0], dr.at[0], at(0, r))

    ag[1, mine] = given - dpiece[...]
    solve(1, lambda: None)

    def left(src, ss, rs, to):
        pltpu.make_async_remote_copy(src_ref=src, dst_ref=src, send_sem=ss, recv_sem=rs, device_id=to, device_id_type=pl.DeviceIdType.MESH).wait_send()

    @pl.loop(0, A)
    def _(m):
        for t in range(2):
            for k in range(1, B):
                n = lax.rem(a + m + 1, A)
                left(pbuf.at[t, flipped(k), n], s1.at[t, k - 1, m], r1.at[t, k - 1, n], plane(k))

    for c in sends:
        c.wait_send()

    @pl.when(i < L - 1)
    def _():
        left(hprev.at[share], hs.at[0], hr.at[0], at(i + 1, r))

    @pl.when(i > 0)
    def _():
        left(cbuf.at[which], gs.at[0], gr.at[0], at(0, r))
        for k in range(1, R):
            left(hprev.at[share], hds.at[k - 1], hdr.at[k - 1], beside(k))


def solution(mesh):
    L, R = mesh.shape["lag"], mesh.shape["row"]
    A, B = split_of(L)

    def shards(blocks, history, excitation, inverse):
        nloc, pr, p = blocks.shape
        steps, _, C = excitation.shape
        q = inverse.shape[0]
        s = pr // L
        G = R if (q // R) % 16 == 0 else 1
        dma = pltpu.SemaphoreType.DMA
        return pl.pallas_call(
            functools.partial(kernel, A, B, R, G),
            out_shape=jax.ShapeDtypeStruct((steps, q, C), F32),
            in_specs=[pl.BlockSpec(memory_space=pl.ANY)] * 4,
            out_specs=pl.BlockSpec(memory_space=pltpu.VMEM),
            scratch_shapes=[
                pltpu.VMEM((nloc, pr, p), BF16),
                pltpu.VMEM((nloc + 1, p, C), BF16),
                pltpu.VMEM((steps, s, C), F32),
                pltpu.VMEM((q, pr), F32),
                pltpu.VMEM((steps, B, A, s, C), F32),
                pltpu.VMEM((steps, B - 1, A, s, C), F32),
                pltpu.VMEM((steps, A, s, C), F32),
                pltpu.VMEM((steps, A - 1, s, C), F32),
                pltpu.VMEM((steps, L, s, C), F32),
                pltpu.VMEM((steps, R, q, C), F32),
                pltpu.VMEM((G, q // G, C), BF16),
                pltpu.VMEM((L, G, q // G, C), BF16),
                pltpu.VMEM((L, s, C), F32),
                pltpu.VMEM((s, C), F32),
                dma((3,)), dma((B,)), dma((1,)), dma((1,)), dma((R - 1,)), dma((R - 1,)),
                dma((steps, B - 1, A)), dma((steps, B - 1, A)), dma((steps, A - 1)), dma((steps, A - 1)),
                dma((steps, A - 1)), dma((steps, A - 1)), dma((steps, A, B - 1)), dma((steps, A, B - 1)),
                dma((steps, R - 1)), dma((steps, R - 1)),
                dma((1,)), dma((L,)), dma((R - 1, L)), dma((R - 1, L)), dma((L,)), dma((1,)),
            ],
            compiler_params=pltpu.CompilerParams(collective_id=0, has_side_effects=True, vmem_limit_bytes=60 * 1024 * 1024),
        )(blocks, history, excitation.reshape(steps, L, s, C), inverse)

    return jax.shard_map(
        shards,
        mesh=mesh,
        in_specs=(P("lag", "row", None), P("lag", None, None), P(None, "row", None), P("lag", "row")),
        out_specs=P(None, "lag", None),
        check_vma=False,
    )
```

time: 65.8 us -> 67.6 us (1.027)
  Pallas kernels: 64 us -> 65.9 us
    pallas_call x1, Pallas kernels: 64 us -> 65.9 us  [shards(): pl.pallas_call(functools.partial(kernel, A, B, R, G), out_shape=jax.Shape...]
where the time goes in v2:
time: 67.6 us; the launch traced here: 67.5 us
  Pallas kernels  65.9 us (97%)
  local copies, waits for them, and re-layouts  1.57 us (2%)
    pallas_call x1, Pallas kernels, shards(): pl.pallas_call(functools.partial(kernel, A, B, R, G), out_shape=jax.Shape...  65.9 us
    unnamed x1, local copies, waits for them, and re-layouts  1.57 us

profile of v2, /device:TPU:7, one launch (start us, length us, event | category | flops | bytes accessed | tf_op | source)
XLA Modules:
  0.0 67.5 jit_solution(5166920908912956444)
XLA Ops:
  0.0 65.9 %shard_map.46 = f32[2,128,128]{2,1,0:T(8,128)} custom-call(bf16[2,1024,2048]{2,1,0:T(8,128)(2,1)} %blocks.1, bf16[2,2048,128]{2,1,0:T(8,128)(2,1)} %history.1, f32[2,16,64,128]{3,2,1,0:T(8,128)} %bitcast.1, f32[128,1024]{1,0:T(8,128)} %inverse.1), custom_call_target="tpu_custom_call" | custom-call | tf_op jit(solution)/shard_map/pallas_call | solution.py:319
  65.9 1.6 %copy.6 = f32[2,128,128]{2,1,0:T(8,128)} copy(f32[2,128,128]{2,1,0:T(8,128)} %shard_map.46) | data formatting | bytes 262144
